TPU v7x, 128 devices: a whole 4x4x4 slice. The times are simulated.
128 devices in a mesh: dp: 1, row: 16 (over z, y), col: 8 (over x, core).
Axes of the slice: x: 4, y: 4, z: 4, core: 2. Of those that a mesh axis runs over, the one named last changes fastest.
Arguments:
- x_in: bfloat16 [16, 512, 4096], P('dp', None, ('row', 'col'))
- ln_gain: bfloat16 [2, 4096], P(None, ('row', 'col'))
- w_in: bfloat16 [2, 4096, 36864], P(None, 'row', 'col')
- w_kv: bfloat16 [2, 4096, 256], P(None, 'row', 'col')
- w_out: bfloat16 [2, 20480, 4096], P(None, 'col', 'row')
Outputs:
- output 1: bfloat16 [16, 512, 4096], P('dp', None, ('row', 'col'))
- output 2: bfloat16 [2, 2, 16, 512, 128], P(None, None, 'dp', ('row', 'col'))
All inputs are finite; a program needn't handle non-finite values.
Results may differ from a plain program's by a relative error of at most 0.0180243.
Values are sent between devices in bfloat16 or wider.
A program may use at most 1 GiB of HBM per device.

v0:
```python
import typing

import jax
import jax.numpy as jnp
import numpy as np
from jax import lax
from jax.experimental import pallas as pl
from jax.experimental.pallas import tpu as pltpu
from jax.sharding import Mesh
from jax.sharding import PartitionSpec as P

LN_EPS = 1e-6
RING = 4
CORES = 2
VMEM_LIMIT = 67_000_000
BF = jnp.bfloat16
F32 = jnp.float32
SLOT_OFF = (2, 1, 3, 0)
SIGN = (1, -1)
NIL = None
BOTH = range(CORES)
RINGS = range(RING)
OTHERS = (1, 3, 2)
LAST = RING - 1
G_ROWS = 8
H_SLOTS = 3
QG0, UP0, WO0, QG1, UP1, WO1 = range(6)
OWN, AFTER, FAR, BEFORE = RINGS
FIRST_ORDER = ("a0", "b0", "a1", "b1", "c0", "c1", "d0", "d1", "e0", "e1")
LAST_ORDER = FIRST_ORDER[:-1] + ("f1", "e1", "g1", "f0", "g0", "h1", "h0")
KINDS = ("first", "second", "first_on", "second_on")


class Refs(typing.NamedTuple):
    xt: typing.Any
    gain_in: typing.Any
    wkv: typing.Any
    w_in: typing.Any
    w_out: typing.Any
    cos_in: typing.Any
    sin_in: typing.Any
    y_out: typing.Any
    kv_out: typing.Any
    h_all: typing.Any
    wi: typing.Any
    wo: typing.Any
    kvh: typing.Any
    kvx: typing.Any
    rwi: typing.Any
    rwo: typing.Any
    cos: typing.Any
    sin: typing.Any
    gain_own: typing.Any
    h_ref: typing.Any
    hid: typing.Any
    gain: typing.Any
    gbuf: typing.Any
    xz: typing.Any
    xp: typing.Any
    wv: typing.Any
    kvb: typing.Any
    wov: typing.Any
    hb: typing.Any
    joined: typing.Any
    qkv: typing.Any
    stage: typing.Any
    lhs: typing.Any
    away: typing.Any
    acc: typing.Any
    die_in: typing.Any
    in1: typing.Any
    in2: typing.Any
    in3: typing.Any
    in4: typing.Any
    xz_send: typing.Any
    xz_recv: typing.Any
    xp_send: typing.Any
    xp_recv: typing.Any
    xd_send: typing.Any
    xd_recv: typing.Any
    x_loc: typing.Any
    g_send: typing.Any
    g_recv: typing.Any
    gd_send: typing.Any
    gd_recv: typing.Any
    yd_send: typing.Any
    yd_recv: typing.Any
    yp_send: typing.Any
    yp_recv: typing.Any
    yz_send: typing.Any
    yz_recv: typing.Any
    y_loc: typing.Any
    ag_send: typing.Any
    ag_recv: typing.Any
    ag_dsend: typing.Any
    ag_drecv: typing.Any
    ag_loc: typing.Any
    h_sem: typing.Any
    kvo_sem: typing.Any
    w_load: typing.Any
    far_load: typing.Any
    y_recv: typing.Any
    ry_recv: typing.Any
    zb_recv: typing.Any
    zc_recv: typing.Any
    w_send: typing.Any
    kz_send: typing.Any
    kz_recv: typing.Any
    ky_send: typing.Any
    ky_recv: typing.Any
    kx_send: typing.Any
    kx_recv: typing.Any
    kd_send: typing.Any
    kd_recv: typing.Any
    k_loc: typing.Any
    dsend: typing.Any
    drecv: typing.Any
    rs_send: typing.Any
    recv1: typing.Any
    recv2: typing.Any
    recv3: typing.Any
    recv4: typing.Any
    small: typing.Any
    kvx_send: typing.Any
    kvx_recv: typing.Any
    kvx_loc: typing.Any


def model_kernel(*refs):
    r = Refs(*refs)
    z, y, x, c = (lax.axis_index(a) for a in ("z", "y", "x", "core"))
    n_layers = r.wkv.shape[0]
    rows, d_model = r.hid.shape
    batch, d_local = r.xt.shape[:2]
    seqs = batch // RING
    seq_len, head_dim = r.cos.shape
    d_row = r.w_in.shape[1]
    e_loc = r.wi.shape[3]
    depth = r.wo.shape[3]
    f_loc = depth - head_dim
    quarter = rows // 4
    width = d_model // RING
    q_block = head_dim * RING
    f_block = f_loc * RING

    turned = {id(v): [lax.rem(v + o, RING) for o in RINGS] for v in (z, y, x)}

    def turn(base, off):
        if isinstance(off, int):
            return turned[id(base)][off % RING]
        return lax.rem(base + off + RING, RING)

    def remote(src, dst, ssem, rsem, dev):
        return pltpu.make_async_remote_copy(
            src_ref=src, dst_ref=dst, send_sem=ssem, recv_sem=rsem, device_id=dev, device_id_type=pl.DeviceIdType.MESH)

    partner = (z, y, x, 1 - c)

    peers = [(turn(z, o), y, x, c) for o in OTHERS]
    peers += [(z, turn(y, oy), turn(x, ox), c) for oy in RINGS for ox in RINGS if oy or ox]
    peers.append(partner)
    here = (z, y, x, c)
    gate_sem = pltpu.get_barrier_semaphore()
    for dev in peers:
        pl.semaphore_signal(gate_sem, inc=1, device_id=dev, device_id_type=pl.DeviceIdType.MESH)
    fills = [pltpu.make_async_copy(src, dst, r.small.at[n]) for n, (src, dst) in enumerate(
        ((r.gain_in, r.gain_own), (r.cos_in, r.cos), (r.sin_in, r.sin)))]
    for fill in fills:
        fill.start()
    fills[0].wait()

    src_id = lax.broadcasted_iota(jnp.int32, (d_local, d_row), 0) + (x * CORES + c) * d_local
    dst_id = lax.broadcasted_iota(jnp.int32, (d_local, d_row), 1)
    spread = jnp.where(src_id == dst_id, 1.0, 0.0).astype(BF)
    r.gbuf[x, c, y, z] = jnp.zeros((G_ROWS, d_row), BF)
    r.gbuf[x, c, y, z, :n_layers] = jnp.dot(r.gain_own[...], spread, preferred_element_type=F32).astype(BF)
    pl.semaphore_wait(gate_sem, len(peers))

    def hook(pump, i):
        with jax.named_scope(f"hook_{i}"):
            pump(i)

    def w_cols(kind):
        return pl.ds(0, head_dim + f_loc) if kind == 0 else pl.ds(head_dim + f_loc, f_loc)

    def piece(t, zz, yy):
        l, kind = t // 3, t % 3
        if kind == 2:
            return r.wo.at[l, zz, yy]
        return r.wi.at[l, zz, pl.ds(pl.multiple_of(yy * d_row, d_row), d_row), w_cols(kind)]

    def piece_half(t, zz, yy, h):
        l, kind = t // 3, t % 3
        if kind == 2:
            return r.wo.at[l, zz, yy, pl.ds(h * (depth // 2), depth // 2)]
        return r.wi.at[l, zz, pl.ds(pl.multiple_of(yy * d_row + h * (d_row // 2), d_row // 2), d_row // 2), w_cols(kind)]

    def own_parts(t, owner, zz, yy):
        l, kind = t // 3, t % 3
        hq = pl.ds(pl.multiple_of(owner * head_dim, head_dim), head_dim)
        if kind == 2:
            return [
                (r.w_out.at[l, hq], r.wo.at[l, zz, yy, pl.ds(0, head_dim)]),
                (r.w_out.at[l, pl.ds(pl.multiple_of(q_block + owner * f_loc, head_dim), f_loc)], r.wo.at[l, zz, yy, pl.ds(head_dim, f_loc)]),
            ]
        rws = pl.ds(pl.multiple_of(yy * d_row, d_row), d_row)
        if kind == 0:
            return [
                (r.w_in.at[l, :, hq], r.wi.at[l, zz, rws, pl.ds(0, head_dim)]),
                (r.w_in.at[l, :, pl.ds(pl.multiple_of(q_block + owner * f_loc, head_dim), f_loc)], r.wi.at[l, zz, rws, pl.ds(head_dim, f_loc)]),
            ]
        return [(r.w_in.at[l, :, pl.ds(pl.multiple_of(q_block + f_block + owner * f_loc, head_dim), f_loc)],
                 r.wi.at[l, zz, rws, pl.ds(head_dim + f_loc, f_loc)])]

    def relay_ref(t, d):
        l, kind = t // 3, t % 3
        return r.rwo.at[l, d] if kind == 2 else r.rwi.at[l, d, :, w_cols(kind)]

    def far_parts(t, d):
        l, kind = t // 3, t % 3
        owner = turn(y, 2)
        hq = pl.ds(pl.multiple_of(owner * head_dim, head_dim), head_dim)
        if kind == 2:
            n = depth // 2
            base = q_block + owner * f_loc
            if d:
                return [(r.w_out.at[l, pl.ds(pl.multiple_of(base + n - head_dim, G_ROWS), n)], r.rwo.at[l, d])]
            return [
                (r.w_out.at[l, hq], r.rwo.at[l, d, pl.ds(0, head_dim)]),
                (r.w_out.at[l, pl.ds(pl.multiple_of(base, head_dim), n - head_dim)], r.rwo.at[l, d, pl.ds(head_dim, n - head_dim)]),
            ]
        rws = pl.ds(d * (d_row // 2), d_row // 2)
        if kind == 0:
            return [
                (r.w_in.at[l, rws, hq], r.rwi.at[l, d, :, pl.ds(0, head_dim)]),
                (r.w_in.at[l, rws, pl.ds(pl.multiple_of(q_block + owner * f_loc, head_dim), f_loc)], r.rwi.at[l, d, :, pl.ds(head_dim, f_loc)]),
            ]
        return [(r.w_in.at[l, rws, pl.ds(pl.multiple_of(q_block + f_block + owner * f_loc, head_dim), f_loc)], relay_ref(t, d))]

    def y_send(t):
        for d in BOTH:
            owner = turn(y, SIGN[d])
            dev = (z, owner, x, c)
            for src, dst in far_parts(t, d):
                remote(src, dst, r.w_send.at[t], r.ry_recv.at[t, d], dev).start()
            for src, dst in own_parts(t, owner, z, y):
                remote(src, dst, r.w_send.at[t], r.y_recv.at[t, -SIGN[d] % RING], dev).start()

    def y_relay(t):
        for d in BOTH:
            ref = relay_ref(t, d)
            remote(ref, ref, r.w_send.at[t], r.ry_recv.at[t, d], here).wait_recv()
            dst = piece_half(t, z, turn(y, -SIGN[d]), d)
            remote(ref, dst, r.w_send.at[t], r.y_recv.at[t, 2], (z, turn(y, SIGN[d]), x, c)).start()

    def z_own(t):
        for d in BOTH:
            for src, dst in own_parts(t, y, z, y):
                remote(src, dst, r.w_send.at[t], r.zb_recv.at[t % 3, 0, d], (turn(z, SIGN[d]), y, x, c)).start()

    def z_direct(t, j):
        yy = turn(y, j)
        ref = piece(t, z, yy)
        remote(ref, ref, r.w_send.at[t], r.y_recv.at[t, j], here).wait_recv()
        for d in BOTH:
            remote(ref, ref, r.w_send.at[t], r.zb_recv.at[t % 3, j, d], (turn(z, SIGN[d]), y, x, c)).start()

    def z_forward(t, j):
        yy = turn(y, j)
        for d in BOTH:
            zz = turn(z, -SIGN[d])
            ref = piece(t, zz, yy)
            remote(ref, ref, r.w_send.at[t], r.zb_recv.at[t % 3, j, d], here).wait_recv()
            part = piece_half(t, zz, yy, d)
            remote(part, part, r.w_send.at[t], r.zc_recv.at[t % 3], (turn(z, SIGN[d]), y, x, c)).start()

    def place(t, zz):
        l, kind = t // 3, t % 3
        if kind == 2:
            return r.wo.at[l, zz], r.wov.at[zz]
        return r.wi.at[l, zz, :, w_cols(kind)], r.wv.at[zz, :, w_cols(kind)]

    def load_near(t):
        kind = t % 3
        for d in BOTH:
            src, dst = place(t, turn(z, SIGN[d]))
            pltpu.make_async_copy(src, dst, r.w_load.at[kind]).start()
        for j in OTHERS:
            yy = turn(y, j)
            dst = r.wov.at[z, yy] if kind == 2 else r.wv.at[z, pl.ds(pl.multiple_of(yy * d_row, d_row), d_row), w_cols(kind)]
            pltpu.make_async_copy(piece(t, z, yy), dst, r.w_load.at[kind]).start()
        for src, dst in own_parts(t, y, z, y):
            pltpu.make_async_copy(src, own_place(t, dst, src), r.w_load.at[kind]).start()

    def load_far(t):
        src, dst = place(t, turn(z, 2))
        remote(src, src, r.w_send.at[t], r.zc_recv.at[t % 3], here).wait_recv()
        pltpu.make_async_copy(src, dst, r.far_load.at[t % 3]).start()

    def own_place(t, dst, src):
        kind = t % 3
        if kind == 2:
            n = src.shape[0]
            return r.wov.at[z, y, pl.ds(0 if n == head_dim and f_loc != head_dim else head_dim, n)]
        n = src.shape[1]
        rws = pl.ds(pl.multiple_of(y * d_row, d_row), d_row)
        if kind == 0:
            return r.wv.at[z, rws, pl.ds(0 if n == head_dim and f_loc != head_dim else head_dim, n)]
        return r.wv.at[z, rws, pl.ds(head_dim + f_loc, f_loc)]

    def near_loaded(t):
        kind = t % 3
        dst = r.wov.at[pl.ds(0, LAST)] if kind == 2 else r.wv.at[pl.ds(0, LAST), :, w_cols(kind)]
        pltpu.make_async_copy(dst, dst, r.w_load.at[kind]).wait()

    def far_loaded(t):
        kind = t % 3
        dst = r.wov.at[0] if kind == 2 else r.wv.at[0, :, w_cols(kind)]
        pltpu.make_async_copy(dst, dst, r.far_load.at[kind]).wait()

    def loaded(t):
        near_loaded(t)
        far_loaded(t)

    def drain(t):
        l, kind = t // 3, t % 3
        ref = r.wo.at[l] if kind == 2 else r.wi.at[l, :, :, w_cols(kind)]
        remote(ref, ref, r.w_send.at[t], r.y_recv.at[t, 0], here).wait_send()

    def kv_z_copy(k):
        return remote(r.wkv, r.kvh.at[x, c, :, y, z], r.kz_send.at[k], r.kz_recv.at[k], (turn(z, OTHERS[k]), y, x, c))

    def kv_own():
        return pltpu.make_async_copy(r.wkv, r.kvh.at[x, c, :, y, z], r.k_loc.at[0])

    def kv_z():
        for k in range(len(OTHERS)):
            kv_z_copy(k).start()
        kv_own().start()

    def kv_y_copy(ref, k, d):
        return remote(ref, ref, r.ky_send, r.ky_recv.at[k], (z, turn(y, SIGN[d]), x, c))

    def kv_y1():
        kv_own().wait()
        for k in range(len(OTHERS)):
            kv_z_copy(k).wait()
        for d in BOTH:
            kv_y_copy(r.kvh.at[x, c, :, y], d, d).start()

    def kv_y2():
        for d in BOTH:
            yy = turn(y, -SIGN[d])
            kv_y_copy(r.kvh.at[x, c, :, yy], d, d).wait_recv()
            kv_y_copy(r.kvh.at[x, c, :, yy, pl.ds(2 * d, 2)], 2, d).start()

    def kv_y3():
        kv_y_copy(r.kvh.at[x, c, :, turn(y, 2)], 2, 0).wait_recv()
        kv_y_copy(r.kvh.at[x, c, :, pl.ds(0, LAST)], 0, 0).wait_send()

    def kv_x_copy(l, ref, k, d):
        return remote(ref, ref, r.kx_send.at[l], r.kx_recv.at[l, k], (z, y, turn(x, SIGN[d]), c))

    def kv_die(l, ref):
        return remote(ref, ref, r.kd_send.at[l], r.kd_recv.at[l], partner)

    def kv_x1(l):
        ref = r.kvh.at[x, c, l]
        for d in BOTH:
            kv_x_copy(l, ref, d, d).start()
        kv_die(l, ref).start()

    def kv_x2(l):
        for d in BOTH:
            xx = turn(x, -SIGN[d])
            ref = r.kvh.at[xx, c, l]
            kv_x_copy(l, ref, d, d).wait_recv()
            kv_x_copy(l, r.kvh.at[xx, c, l, pl.ds(2 * d, 2)], 2, d).start()
            kv_die(l, ref).start()

    def kv_x3(l):
        ref = r.kvh.at[turn(x, 2), c, l]
        kv_x_copy(l, ref, 2, 0).wait_recv()
        kv_die(l, ref).start()

    def kv_load(l):
        kv_die(l, r.kvh.at[:, 1 - c, l]).wait_recv()
        kc = r.wkv.shape[1]
        for xx in RINGS:
            for cc in BOTH:
                pltpu.make_async_copy(r.kvh.at[xx, cc, l], r.kvb.at[:, :, pl.ds((xx * CORES + cc) * kc, kc)], r.k_loc.at[1]).start()

    def kv_sent(l):
        kv_x_copy(l, r.kvh.at[pl.ds(0, LAST), c, l], 0, 0).wait_send()
        kv_die(l, r.kvh.at[:, c, l]).wait_send()

    def kv_loaded():
        pltpu.make_async_copy(r.kvb, r.kvb, r.k_loc.at[1]).wait()

    def gain_move(i, src, dst, dev):
        return remote(src, dst, r.g_send.at[i], r.g_recv.at[i], dev)

    def gain_z(k):
        dev = (turn(z, OTHERS[k]), y, x, c)
        return gain_move(k, r.gbuf.at[x, c, y, z], r.gbuf.at[x, c, y, z], dev)

    def gain_y(k):
        dev = (z, turn(y, OTHERS[k]), x, c)
        return gain_move(len(OTHERS) + k, r.gbuf.at[x, c, y], r.gbuf.at[x, c, y], dev)

    def gain_x(k):
        dev = (z, y, turn(x, OTHERS[k]), c)
        return gain_move(CORES * len(OTHERS) + k, r.gbuf.at[x, c], r.gbuf.at[x, c], dev)

    def gain_die(xx, k):
        ref = r.gbuf.at[xx, c]
        return remote(ref, ref, r.gd_send.at[k], r.gd_recv.at[k], partner)

    def gain_sum():
        for zz in RINGS:
            for yy in RINGS:
                tot = jnp.zeros((n_layers, d_row), F32)
                for xx in RINGS:
                    for cc in BOTH:
                        tot += r.gbuf[xx, cc, yy, zz, :n_layers].astype(F32)
                at = (zz * RING + yy) * d_row
                r.gain[:, at:at + d_row] = tot

    tok_pair = CORES * rows

    def x_z(k):
        zz = turn(z, OTHERS[k])
        src = r.xt.at[pl.ds(zz * seqs, seqs)]
        return remote(src, r.xz.at[z], r.xz_send, r.xz_recv, (zz, y, x, c))

    def three_planes():
        ref = r.xz.at[pl.ds(0, LAST)]
        return remote(ref, ref, r.xz_send, r.xz_recv, here)

    def x_own():
        return pltpu.make_async_copy(r.xt.at[pl.ds(z * seqs, seqs)], r.xz.at[z], r.x_loc)

    def pos(xx):
        return pl.ds(pl.multiple_of(xx * tok_pair, tok_pair), tok_pair)

    def x_plane(oy, ox):
        yy, xx = turn(y, oy), turn(x, ox)
        return remote(r.xz.at[:, yy, :, pos(xx)], r.xp.at[c, y, x], r.xp_send.at[oy], r.xp_recv.at[(RING - oy) % RING], (z, yy, xx, c))

    def row_bytes(oy):
        return r.xp.at[c, 0] if oy else r.xp.at[c, 0, pl.ds(0, RING - 1)]

    def x_row(oy):
        yy = turn(y, oy)
        got = row_bytes(oy)
        remote(got, got, r.xp_send.at[oy], r.xp_recv.at[oy], partner).wait_recv()
        row = r.xp.at[c, yy]
        remote(row, row, r.xd_send, r.xd_recv, partner).start()

    def x_turn():
        got = r.xp.at[1 - c]
        remote(got, got, r.xd_send, r.xd_recv, partner).wait_recv()

        @pl.loop(0, RING)
        def _(zz):
            for yy in RINGS:
                for xh in BOTH:
                    blk = [r.xp[cc, yy, CORES * xh + xx, zz] for xx in BOTH for cc in BOTH]
                    blk = jnp.concatenate(blk, axis=0).astype(F32).T.astype(BF)
                    n = blk.shape[1]
                    at = pl.multiple_of(zz * RING * d_row + yy * d_row + xh * n, n)
                    r.hb[0, 0, :, :, pl.ds(at, n)] = blk.reshape(CORES, rows, n)
        r.hid[...] = r.hb[0, 0, c]
        remote(got, got, r.xd_send, r.xd_recv, partner).wait_send()

    def x_sent():
        three_planes().wait_send()
        for fn in (gain_z, gain_y, gain_x):
            peers_of(fn, "wait_send")
        for k in RINGS:
            gain_die(x, k).wait_send()
        for oy in RINGS:
            got = row_bytes(oy)
            remote(got, got, r.xp_send.at[oy], r.xp_recv.at[oy], partner).wait_send()

    def y_die(p):
        cols = pl.ds(pl.multiple_of(turn(z, p) * width, width), width)
        return remote(r.hid.at[:, cols], r.hb.at[0, 0, c, :, cols], r.yd_send.at[p], r.yd_recv.at[p], partner)

    def planes(h):
        return pl.ds(2 * h, 2)

    def y_plane(h, oy, ox):
        yy, xx = turn(y, oy), turn(x, ox)
        return remote(r.xp.at[c, yy, xx, planes(h)], r.xz.at[planes(h), y, :, pos(x)], r.yp_send.at[h, oy], r.yp_recv.at[h, (RING - oy) % RING],
                      (z, yy, xx, c))

    def y_z(p, oy):
        s = turn(y, oy)
        return remote(r.xz.at[p, s], r.y_out.at[z * seqs + s], r.yz_send.at[p], r.yz_recv.at[p], (turn(z, p), y, x, c))

    def y_own(oy):
        s = turn(y, oy)
        return pltpu.make_async_copy(r.xz.at[0, s], r.y_out.at[z * seqs + s], r.y_loc)

    def leave_a(h):
        for p in BOTH:
            p = 2 * h + p
            y_die(p).start()
            cols = pl.ds(pl.multiple_of(turn(z, p) * width, width), width)
            r.hb[0, 0, c, :, cols] = r.hid[:, cols]

    def leave_b(h):
        n = CORES * CORES * d_local
        for p in BOTH:
            p = 2 * h + p
            y_die(p).wait()

            @pl.loop(0, RING)
            def _(yy, p=p):
                for xh in BOTH:
                    at = pl.multiple_of(turn(z, p) * width + yy * d_row + xh * n, n)
                    blk = r.hb[0, 0, :, :, pl.ds(at, n)].reshape(tok_pair, n).astype(F32).T.astype(BF)
                    for xx in BOTH:
                        for cc in BOTH:
                            lo = (xx * CORES + cc) * d_local
                            r.xp[cc, yy, CORES * xh + xx, p] = blk[lo:lo + d_local]

        for oy in OTHERS + (0,):
            for ox in RINGS:
                if oy or ox:
                    y_plane(h, oy, ox).start()
        for p in BOTH:
            p = 2 * h + p
            r.xz[p, y, :, pos(x)] = r.xp[c, y, x, p]

    def plane_bytes(h, oy):
        return r.xp.at[c, 0, :, planes(h)] if oy else r.xp.at[c, 0, pl.ds(0, LAST), planes(h)]

    def leave_c(h):
        for oy in OTHERS + (0,):
            got = plane_bytes(h, oy)
            remote(got, got, r.yp_send.at[h, oy], r.yp_recv.at[h, oy], partner).wait_recv()
            for p in BOTH:
                p = 2 * h + p
                (y_z(p, oy) if p else y_own(oy)).start()

    def left():
        for oy in RINGS:
            for h in BOTH:
                got = plane_bytes(h, oy)
                remote(got, got, r.yp_send.at[h, oy], r.yp_recv.at[h, oy], partner).wait_send()
        for p in OTHERS:
            ref = r.xz.at[p]
            remote(ref, ref, r.yz_send.at[p], r.yz_recv.at[p], here).wait()
        pltpu.make_async_copy(r.xz.at[0], r.xz.at[0], r.y_loc).wait()

    def kv_rows(zz):
        n = CORES * seq_len // (RING * RING * RING * CORES)
        return pl.ds(pl.multiple_of(((zz * RING + y) * RING + x) * n, n), n)

    def kv_trade(l, k):
        zz = turn(z, OTHERS[k])
        return remote(r.kv_out.at[l, :, :, kv_rows(zz)], r.kvx.at[l, z], r.kvx_send.at[l, k], r.kvx_recv.at[l, k], (zz, y, x, c))

    def kv_keep(l):
        return pltpu.make_async_copy(r.kv_out.at[l, :, :, kv_rows(z)], r.kvx.at[l, z], r.kvx_loc.at[l])

    def kv_share(l):
        for k in range(len(OTHERS)):
            kv_trade(l, k).start()
        kv_keep(l).start()

    def kv_shared(l):
        for k in range(len(OTHERS)):
            kv_trade(l, k).wait()
        kv_keep(l).wait()

    def gather_norm(l, split, pump):
        hid = r.hid
        gain = r.gain[l:l + 1, :]
        for b in range(4):
            blk = hid[b * quarter:(b + 1) * quarter, :].astype(F32)
            mean = jnp.mean(blk, axis=-1, keepdims=True)
            cen = blk - mean
            var = jnp.mean(cen * cen, axis=-1, keepdims=True)
            r.h_ref[b * quarter:(b + 1) * quarter, :] = (cen * lax.rsqrt(var + LN_EPS) * gain).astype(BF)
        out = r.h_all.at[l]

        def spot(q, first, second):
            if q == 0:
                return turn(y, second), turn(x, first)
            return turn(y, first), turn(x, second)

        def span(q, part):
            lo, n = (split, rows - split) if q else (0, split)
            if part is NIL:
                return pl.ds(lo, n)
            return pl.ds(lo + part * (n // 2), n // 2)

        offs = (0, -1, 1, 2)
        plans = {}
        for q in BOTH:
            for d in BOTH:
                plans["first", q, d] = (q, 0, 0, NIL, SIGN[d], 0)
                plans["first_on", q, d] = (q, -SIGN[d], 0, d, SIGN[d], 0)
                for k in RINGS:
                    plans["second", q, k, d] = (q, offs[k], 0, NIL, 0, SIGN[d])
                    plans["second_on", q, k, d] = (q, offs[k], -SIGN[d], d, 0, SIGN[d])
        index = {key: n for n, key in enumerate(plans)}

        def link(*key, own=False):
            idx, (q, first, second, part, to_first, to_second) = index[key], plans[key]
            sy, sx = spot(q, first, second)
            ty, tx = spot(q, to_first, to_second)
            rws = span(q, part)
            dst = out.at[sy, sx, c, rws]
            return remote(r.h_ref.at[rws] if own else dst, dst, r.ag_send.at[KINDS.index(key[0])], r.ag_recv.at[idx], (z, ty, tx, c))

        def arrived(*key):
            for d in BOTH:
                link(*key, d).wait_recv()

        def die(q, first, second, own=False):
            sy, sx = spot(q, first, second)
            rws = span(q, NIL)
            dst = out.at[sy, sx, c, rws]
            off = (first if q else second) % RING
            remote(r.h_ref.at[rws] if own else dst, dst, r.ag_dsend, r.ag_drecv.at[off], partner).start()

        def take(k, q):
            for d in BOTH:
                link("second", q, k, d).wait_recv()
                die(q, offs[k], -SIGN[d])

        def pass_on(k, q):
            for d in BOTH:
                link("second_on", q, k, d).start()

        def second_step(k):
            take(k, 1)
            pass_on(k, 1)
            take(k, 0)

        def far_first(q):
            for e in BOTH:
                link("second", q, LAST, e).start()

        def last_step(q, k):
            arrived("second_on", q, k)
            die(q, offs[k], 2)

        def tail_a():
            second_step(2)
            far_first(1)
            for k in RINGS[:-1]:
                pass_on(k, 0)
            hook(pump, "k2")
            take(LAST, 0)
            pass_on(LAST, 0)
            hook(pump, "k3")
            for k in (1, 2):
                last_step(1, k)

        def tail_b():
            take(LAST, 1)
            pass_on(LAST, 1)

        def tail_c():
            for k in RINGS:
                last_step(0, k)
            last_step(1, LAST)

        for q in BOTH:
            for d in BOTH:
                link("first", q, d, own=True).start()
        for q in BOTH:
            for d in BOTH:
                link("second", q, 0, d, own=True).start()
        for q in BOTH:
            die(q, 0, 0, own=True)
        own = pltpu.make_async_copy(r.h_ref, out.at[y, x, c], r.ag_loc)
        own.start()
        hook(pump, "begin")
        for d in BOTH:
            for q in BOTH:
                link("first", q, d).wait_recv()
                src = -SIGN[d]
                link("first_on", q, d).start()
                die(q, src, 0)
        hook(pump, "first")
        second_step(0)
        for q in reversed(BOTH):
            for d in BOTH:
                for e in BOTH:
                    link("second", q, 1 + d, e).start()
        hook(pump, "k0")
        for q in BOTH:
            arrived("first_on", q)
            die(q, 2, 0)
        far_first(0)
        hook(pump, "first_on")
        last_step(1, 0)
        own.wait()
        hook(pump, "ready")

        def crossed(off):
            got = out.at[turn(y, off), :, 1 - c]
            remote(got, got, r.ag_dsend, r.ag_drecv.at[off], partner).wait_recv()

        def order(i):
            if isinstance(i, int):
                return (OWN, BEFORE, AFTER, FAR)[i]
            return lax.rem(3 * i + 3 * (i // 2) + 2 * (i // 3), RING)

        def fetch(i, slot):
            off = order(i)
            crossed(off)
            h_copy(l, turn(y, off), slot).start()

        def up_ready():
            hook(pump, "up")
            loaded(UP1 if l else UP0)

        crossed(0)
        h_copy(l, y, 0).start()

        def opening():
            second_step(1)
            hook(pump, "k1")

        def turn_of(i):
            slot = lax.rem(i, H_SLOTS)
            s = turn(y, order(i))
            h_copy(l, s, slot).wait()
            pump(("seq", i))
            one(l, s, slot, i)

            @pl.when(i == 1)
            def _():
                tail_b()

            @pl.when(i == 2)
            def _():
                tail_c()
                fetch(LAST, 0)

            return s, slot

        def neighbours():
            tail_a()
            for n in (1, 2):
                fetch(n, n)

        if l:
            @pl.loop(0, RING)
            def _(i):
                s, slot = turn_of(i)

                @pl.when(i == 0)
                def _():
                    opening()
                    up_ready()

                pump(("two", i))
                two(s, slot)

                @pl.when(i == 0)
                def _():
                    neighbours()
        else:
            h_copy(l, y, 0).wait()
            hook(pump, "own")
            one(l, y, 0, 0)
            opening()
            neighbours()

            @pl.loop(1, RING)
            def _(i):
                turn_of(i)

                @pl.when(i == 1)
                def _():
                    up_ready()

                pump(("two", i - 1))
                two(turn(y, order(i - 1)), lax.rem(i - 1, H_SLOTS))

            hook(pump, "two3")
            two(turn(y, FAR), 0)

        for slot in BOTH:
            for i in BOTH:
                kv_out_copy(l, 0, slot, i).wait()
        sent = (out.at[y, x], out.at[y], out.at[y, x, c], out.at[y, pl.ds(0, CORES)])
        for kind, ref in enumerate(sent):
            remote(ref, ref, r.ag_send.at[kind], r.ag_recv.at[kind], partner).wait_send()
        remote(out.at[pl.ds(0, 2)], out.at[pl.ds(0, 2)], r.ag_dsend, r.ag_drecv.at[0], partner).wait_send()

    def h_copy(l, s, slot):
        return pltpu.make_async_copy(r.h_all.at[l, s], r.hb.at[slot], r.h_sem.at[slot])

    def h_tile(slot):
        return r.hb[slot].reshape(seq_len, d_model)

    def project(h, lo, n):
        w = r.wv[:, :, lo:lo + n].reshape(d_model, n)
        return jnp.dot(h, w, preferred_element_type=F32).astype(BF)

    def rope(val):
        val = val.astype(F32)
        return val * r.cos[...] + pltpu.roll(val, head_dim // 2, 1) * r.sin[...]

    n_chunk = min(256, f_loc)

    def kv_out_copy(l, s, slot, i):
        return pltpu.make_async_copy(r.qkv.at[slot, i], r.kv_out.at[l, i, s], r.kvo_sem.at[slot, i])

    def one(l, s, slot, i):
        pair = i % 2 if isinstance(i, int) else lax.rem(i, 2)

        @pl.when(i >= 2)
        def _():
            for k in BOTH:
                kv_out_copy(l, s, pair, k).wait()

        kv = jnp.zeros((seq_len, 2 * head_dim), F32)
        for zz in RINGS:
            for yy in RINGS:
                col = (zz * RING + yy) * d_row
                kv += lax.dot_general(h_cols(slot, col, d_row), r.kvb[yy, zz], (((1,), (1,)), ((), ())), preferred_element_type=F32)
        kv = kv.astype(BF)
        r.qkv[pair, 0] = rope(kv[:, :head_dim]).astype(BF)
        r.qkv[pair, 1] = kv[:, head_dim:]
        for i in BOTH:
            kv_out_copy(l, s, pair, i).start()
        q = project(h_tile(slot), 0, head_dim)
        r.stage[...] = (rope(q) * head_dim ** -0.5).astype(BF)
        for lo in range(0, f_loc, n_chunk):
            r.joined[s, :, head_dim + lo:head_dim + lo + n_chunk] = project(h_tile(slot), head_dim + lo, n_chunk)
        n_tile = seq_len // 2
        for i in BOTH:
            keys = (i + 1) * n_tile
            sc = lax.dot_general(r.stage[i * n_tile:(i + 1) * n_tile, :], r.qkv[pair, 0, :keys, :], (((1,), (1,)), ((), ())), preferred_element_type=F32)
            row_id = lax.broadcasted_iota(jnp.int32, sc.shape, 0) + i * n_tile
            col_id = lax.broadcasted_iota(jnp.int32, sc.shape, 1)
            sc = jnp.where(col_id <= row_id, sc, -1e30)
            top = jnp.max(sc, axis=-1, keepdims=True)
            ex = jnp.exp(sc - top)
            prob = (ex * (1.0 / jnp.sum(ex, axis=-1, keepdims=True))).astype(BF)
            att = jnp.dot(prob, r.qkv[pair, 1, :keys, :], preferred_element_type=F32)
            r.joined[s, i * n_tile:(i + 1) * n_tile, :head_dim] = att.astype(BF)

    def h_cols(slot, col, n):
        return r.hb[slot, :, :, :, col:col + n].reshape(seq_len, n)

    def two(s, slot):
        for lo in range(0, f_loc, n_chunk):
            up = project(h_tile(slot), head_dim + f_loc + lo, n_chunk).astype(F32)
            cols = slice(head_dim + lo, head_dim + lo + n_chunk)
            g = r.joined[s, :, cols].astype(F32)
            r.joined[s, :, cols] = (g * jax.nn.sigmoid(g) * up).astype(BF)

    def out_scatter(l, pump):
        def peer(q, first, second):
            dy = first * (1 - q) + second * q
            dx = first * q + second * (1 - q)
            return (z, turn(y, dy), turn(x, dx), c)

        def die_copy(ch, q, s):
            return remote(r.away.at[q], r.die_in.at[ch, q, s], r.dsend.at[q], r.drecv.at[ch, q, s], partner)

        def first_copy(ch, q, d):
            return remote(r.acc.at[ch, q, 0, pl.ds(CORES * d, CORES)], r.in1.at[ch, q, d], r.rs_send.at[0], r.recv1.at[ch, q, d],
                          peer(q, SIGN[d], 0))

        def second_copy(ch, q, d, h):
            js = pl.ds(CORES * h, CORES)
            return remote(r.acc.at[ch, q, 1 + d, js], r.in2.at[ch, q, d, js], r.rs_send.at[1], r.recv2.at[ch, q],
                          peer(q, SIGN[d], 0))

        def half_rows(d):
            return pl.ds(d * (rows // 2), rows // 2)

        def third_copy(ch, q, d):
            return remote(r.acc.at[ch, q, LAST, 0, half_rows(d)], r.in3.at[ch, q, d], r.rs_send.at[2], r.recv3.at[ch, q, d],
                          peer(q, 0, SIGN[d]))

        def fourth_copy(ch, q, d):
            return remote(r.acc.at[ch, q, LAST, 1 + d], r.in4.at[ch, q, d], r.rs_send.at[LAST], r.recv4.at[ch, q],
                          peer(q, 0, SIGN[d]))

        n_blk = r.wov.shape[3]

        def plane_of(ch, q):
            if l:
                return turn(z, q if ch else 2 + q)
            return turn(z, LAST - q if ch else q)

        def slot_off(s):
            return lax.rem(2 + 3 * s + 3 * (s // 2) + 2 * (s // 3), RING)

        def tile(ch, q, s):
            off = slot_off(s)
            for cc in BOTH:
                for j in RINGS:
                    oy = off * (1 - q) + SLOT_OFF[j] * q
                    ox = SLOT_OFF[j] * (1 - q) + off * q
                    core = c if cc else 1 - c
                    at = pl.multiple_of((turn(x, ox) * CORES + core) * rows, rows)
                    r.lhs[pl.ds((cc * RING + j) * rows, rows), :] = r.joined[turn(y, oy), pl.ds(at, rows), :]
            left = r.lhs[...]
            zz = plane_of(ch, q)
            for n in RINGS:
                res = jnp.dot(left, r.wov[zz, n], preferred_element_type=F32).astype(BF)
                res = res.reshape(CORES, RING, rows, n_blk)
                r.away[q, :, :, n * n_blk:(n + 1) * n_blk] = res[0]
                r.acc[ch, q, s, :, :, n * n_blk:(n + 1) * n_blk] = res[1]

        def pair_sum(ch, q, s):
            die_copy(ch, q, s).wait_recv()

            @pl.loop(0, RING)
            def _(j):
                r.acc[ch, q, s, j] = r.acc[ch, q, s, j] + r.die_in[ch, q, s, j]

        def stage_a(ch):
            @pl.loop(0, CORES * RING)
            def _(t):
                s = t // CORES
                q = lax.rem(t, CORES)

                @pl.when(s >= 1)
                def _():
                    die_copy(ch, q, s - 1).wait_send()

                if ch:
                    @pl.when(s == 0)
                    def _():
                        die_copy(ch - 1, q, LAST).wait_send()

                tile(ch, q, s)
                die_copy(ch, q, s).start()

                @pl.when(s >= 1)
                def _():
                    pair_sum(ch, q, s - 1)

                @pl.when(s == 1)
                def _():
                    for d in BOTH:
                        first_copy(ch, q, d).start()

                for d in BOTH:
                    @pl.when(s == 2 + d)
                    def _(d=d):
                        second_copy(ch, q, d, 1 - d).start()

                for n in RINGS:
                    name = f"a{ch}s{n}"
                    if pump(name, False):
                        @pl.when(t == CORES * n + 1)
                        def _(name=name):
                            hook(pump, name)

        def stage_b(ch):
            for q in BOTH:
                pair_sum(ch, q, LAST)
            for q in BOTH:
                for d in BOTH:
                    first_copy(ch, q, d).wait_recv()
                    for j in BOTH:
                        at = CORES * d + j
                        r.acc[ch, q, 1 + d, at] = r.acc[ch, q, 1 + d, at] + r.in1[ch, q, d, j]
                    second_copy(ch, q, d, d).start()

        def total(ch, q, j):
            val = r.acc[ch, q, LAST, j].astype(F32)
            for d in BOTH:
                val += r.in2[ch, q, d, j].astype(F32)
            r.acc[ch, q, LAST, j] = val.astype(BF)

        def stage_c(ch):
            for q in BOTH:
                ref = r.in2.at[ch, q]
                remote(ref, ref, r.rs_send.at[1], r.recv2.at[ch, q], here).wait_recv()
                total(ch, q, 0)
                for d in BOTH:
                    third_copy(ch, q, d).start()
                for j in RINGS[1:]:
                    total(ch, q, j)

        def stage_d(ch):
            for q in BOTH:
                for d in BOTH:
                    third_copy(ch, q, d).wait_recv()
                    rws = half_rows(d)
                    r.acc[ch, q, LAST, 1 + d, rws] = r.acc[ch, q, LAST, 1 + d, rws] + r.in3[ch, q, d]
                    fourth_copy(ch, q, d).start()

        def stage_e(ch):
            for q in BOTH:
                ref = r.in4.at[ch, q]
                remote(ref, ref, r.rs_send.at[LAST], r.recv4.at[ch, q], here).wait_recv()
                cols = pl.ds(pl.multiple_of(plane_of(ch, q) * width, width), width)
                upd = r.acc[ch, q, LAST, LAST].astype(F32)
                for d in BOTH:
                    upd += r.in4[ch, q, d].astype(F32)
                upd = upd.astype(BF)
                r.hid[:, cols] = (r.hid[:, cols].astype(F32) + upd.astype(F32)).astype(BF)

        stages = {"a": stage_a, "b": stage_b, "c": stage_c, "d": stage_d, "e": stage_e, "f": leave_a, "g": leave_b, "h": leave_c}
        for step in LAST_ORDER if l else FIRST_ORDER:
            with jax.named_scope(step):
                stages[step[0]](int(step[1]))
            hook(pump, step)
        for q in BOTH:
            die_copy(1, q, LAST).wait_send()
        for n, ref in enumerate((r.in1, r.in2, r.in3, r.in4)):
            remote(ref, ref, r.rs_send.at[n], r.drecv.at[0, 0, 0], here).wait_send()

    def near(fn, t):
        for j in (LAST, 1):
            fn(t, j)

    def far(fn, t):
        fn(t, 2)

    def z_all(t):
        near(z_direct, t)
        far(z_direct, t)

    def peers_of(fn, op="start"):
        for k in range(len(OTHERS)):
            getattr(fn(k), op)()

    def start(pump):
        peers_of(gain_z)
        kv_z()
        peers_of(x_z)
        x_own().start()
        pump("s0")
        with jax.named_scope("gain_a"):
            peers_of(gain_z, "wait_recv")
            peers_of(gain_y)
            kv_y1()
        pump("s1")
        with jax.named_scope("gain_b"):
            peers_of(gain_y, "wait_recv")
            peers_of(gain_x)
            gain_die(x, LAST).start()
        pump("s2")
        with jax.named_scope("x_z"):
            three_planes().wait_recv()
            x_own().wait()
        for oy in RINGS:
            for ox in RINGS:
                if oy or ox:
                    x_plane(oy, ox).start()
        r.xp[c, y, x] = r.xz[:, y, :, pos(x)]
        pump("s3")
        with jax.named_scope("kv_b"):
            kv_y2()
        with jax.named_scope("gain_c"):
            for k, o in enumerate(OTHERS):
                gain_x(k).wait_recv()
                gain_die(turn(x, -o), k).start()
        pump("s4")
        for oy in (OWN, BEFORE, AFTER, FAR):
            with jax.named_scope(f"row_{oy}"):
                x_row(oy)
            pump(f"r{oy}")
        pump("s5")
        kv_y3()
        pump("s6")
        with jax.named_scope("gain_sum"):
            for k in RINGS:
                gain_die(x, k).wait_recv()
            gain_sum()
            for fill in fills[1:]:
                fill.wait()
        with jax.named_scope("turn"):
            x_turn()
        pump("s7")

    def when(i, n, *fns):
        @pl.when(i == n)
        def _():
            for fn in fns:
                fn()

    def plan(steps):
        def pump(step, run=True):
            if not isinstance(step, str):
                for n in RINGS:
                    if (step[0], n) in steps:
                        when(step[1], n, lambda n=n: run_steps(steps[step[0], n]))
                return True
            found = steps.get(step, ())
            if run:
                run_steps(found)
            return found
        return pump

    def run_steps(steps):
        for fn, *args in steps:
            with jax.named_scope(f"{fn.__name__}_{args[-1] if args else 0}"):
                fn(*args)

    first_entry = plan({
        "s0": [(z_own, UP0)],
        "s1": [(y_send, QG0)],
        "s3": [(z_own, QG0)],
        "r0": [(y_relay, QG0), (z_forward, UP0, OWN), (z_direct, QG0, AFTER), (z_forward, QG0, OWN), (z_direct, QG0, BEFORE)],
        "s6": [(kv_x1, 0)],
    })
    first_front = plan({
        "begin": [(kv_x2, 0), (y_send, UP0), (z_forward, QG0, AFTER), (z_direct, QG0, FAR)],
        "k0": [(y_relay, UP0), (kv_x3, 0), (z_forward, QG0, BEFORE), (z_forward, QG0, FAR), (z_direct, UP0, AFTER), (z_direct, UP0, BEFORE)],
        "first_on": [(y_send, WO0)],
        "ready": [(load_near, QG0), (load_far, QG0), (kv_load, 0), (loaded, QG0), (kv_loaded,)],
        "k1": [(z_direct, UP0, FAR), (z_forward, UP0, AFTER)],
        "k2": [
            (z_forward, UP0, BEFORE), (y_relay, WO0), (z_forward, UP0, FAR), (y_send, QG1), (z_own, WO0), (z_direct, WO0, BEFORE),
            (kv_x1, 1),
        ],
        ("seq", 1): [(y_send, WO1), (z_direct, WO0, AFTER), (x_sent,)],
        "up": [(y_send, UP1), (z_direct, WO0, FAR), (load_near, UP0), (load_far, UP0)],
        ("two", 0): [(y_relay, QG1), (z_forward, WO0, OWN)],
        ("seq", 2): [(kv_x2, 1)],
        ("two", 1): [(kv_x3, 1), (z_direct, QG1, AFTER), (z_forward, WO0, BEFORE)],
        ("seq", 3): [(y_relay, WO1), (z_forward, WO0, AFTER)],
        ("two", 2): [(z_forward, WO0, FAR), (z_own, QG1), (y_relay, UP1)],
        "near": [(load_near, WO0)],
    })
    first_scatter = plan({
        "a0s0": [(z_forward, QG1, AFTER)],
        "a0s2": [(z_direct, QG1, BEFORE)],
        "b0": [(load_far, WO0), (far_loaded, WO0)],
        "a1s0": [(z_direct, QG1, FAR)],
        "a1s1": [(z_forward, QG1, OWN)],
        "a1": [(z_direct, UP1, FAR)],
        "b1": [(z_direct, UP1, BEFORE)],
        "c1": [(z_forward, QG1, FAR), (z_direct, UP1, AFTER), (z_own, UP1), (z_forward, QG1, BEFORE)],
        "e0": [(z_forward, UP1, FAR)],
    })
    second_front = plan({
        "begin": [(z_forward, UP1, BEFORE), (kv_load, 1)],
        "first": [(z_forward, UP1, AFTER)],
        "k0": [(z_forward, UP1, OWN), (z_direct, WO1, FAR)],
        "ready": [(load_near, QG1), (load_far, QG1), (loaded, QG1), (kv_loaded,)],
        ("seq", 0): [(z_own, WO1)],
        "k1": [(z_direct, WO1, BEFORE)],
        "up": [(load_near, UP1), (load_far, UP1)],
        "k2": [(z_direct, WO1, AFTER)],
        ("seq", 1): [(z_forward, WO1, FAR)],
        ("two", 1): [(z_forward, WO1, OWN)],
        ("two", 2): [(z_forward, WO1, BEFORE), (z_forward, WO1, AFTER)],
        "near": [(load_near, WO1), (load_far, WO1)],
    })
    second_scatter = plan({
    })

    with jax.named_scope("start"):
        start(first_entry)
    with jax.named_scope("front_0"):
        gather_norm(0, rows // RING, first_front)
    with jax.named_scope("near_0"):
        kv_share(0)
        first_front("near")
        near_loaded(WO0)
    with jax.named_scope("scatter_0"):
        out_scatter(0, first_scatter)
    with jax.named_scope("front_1"):
        gather_norm(1, rows // 2, second_front)
    with jax.named_scope("near_1"):
        kv_share(1)
        second_front("near")
        loaded(WO1)
    with jax.named_scope("scatter_1"):
        out_scatter(1, second_scatter)
    with jax.named_scope("drain"):
        left()
        for t in range(WO1 + 1):
            drain(t)
        for l in range(n_layers):
            kv_shared(l)
            kv_sent(l)


def run_model(xt, gain, wkv_t, w_in, w_out, cos_full, sin_full):
    batch, d_local, seq_len = xt.shape
    n_layers, d_row, e_block = w_in.shape
    r_block, d_col = w_out.shape[1:]
    head_dim = cos_full.shape[1]
    d_model = d_row * RING * RING
    seqs = batch // RING
    rows = seqs * seq_len // (RING * RING * CORES)
    e_loc, r_loc = e_block // RING, r_block // RING
    kc = wkv_t.shape[1]
    width = d_model // RING
    n_t = 3 * n_layers
    n_o = len(OTHERS)

    def dma(*shape):
        return pltpu.SemaphoreType.DMA(shape)

    def vm(*shape):
        return pltpu.VMEM(shape, BF)

    def out(*shape):
        return jax.ShapeDtypeStruct(shape, BF)

    any_spec = pl.BlockSpec(memory_space=pl.ANY)
    out_shape = [
        out(batch, d_local, seq_len),
        out(n_layers, 2, seqs, seq_len, head_dim),
        out(n_layers, RING, RING, CORES, rows, d_model),
        out(n_layers, RING, RING * d_row, e_loc),
        out(n_layers, RING, RING, r_loc, d_col),
        out(RING, CORES, n_layers, RING, RING, kc, d_row),
        out(n_layers, RING, 2, seqs, CORES * (seq_len // (CORES * RING * RING * RING)), head_dim),
        out(n_layers, 2, d_row // 2, e_loc),
        out(n_layers, 2, r_loc // 2, d_col),
    ]
    pair = (2, 2, 2)
    scratch = [
        pltpu.VMEM(cos_full.shape, F32), pltpu.VMEM(cos_full.shape, F32), vm(n_layers, d_local),
        vm(rows, d_model), vm(rows, d_model), pltpu.VMEM((n_layers, d_model), F32),
        vm(RING, CORES, RING, RING, G_ROWS, d_row),
        vm(RING, seqs, d_local, seq_len),
        vm(CORES, RING, RING, RING, d_local, CORES * rows),
        vm(RING, RING * d_row, e_loc), vm(RING, RING, 2 * head_dim, d_row), vm(RING, RING, r_loc, d_col),
        vm(H_SLOTS, RING, CORES, rows, d_model), vm(RING, seq_len, r_loc), vm(2, 2, seq_len, head_dim), vm(seq_len, head_dim),
        vm(CORES * RING * rows, r_loc), vm(2, RING, rows, width), vm(2, 2, RING, RING, rows, width), vm(2, 2, RING, RING, rows, width),
        vm(*pair, 2, rows, width), vm(*pair, RING, rows, width), vm(*pair, rows // 2, width), vm(*pair, rows, width),
        pltpu.SemaphoreType.DMA, pltpu.SemaphoreType.DMA, dma(RING), dma(RING), pltpu.SemaphoreType.DMA, pltpu.SemaphoreType.DMA,
        pltpu.SemaphoreType.DMA,
        dma(3 * n_o), dma(3 * n_o), dma(RING), dma(RING),
        dma(RING), dma(RING), dma(2, RING), dma(2, RING), dma(RING), dma(RING), pltpu.SemaphoreType.DMA,
        dma(RING), dma(40), pltpu.SemaphoreType.DMA, dma(RING), pltpu.SemaphoreType.DMA, dma(H_SLOTS), dma(2, 2), dma(3), dma(3),
        dma(n_t, RING), dma(n_t, 2), dma(3, RING, 2), dma(3), dma(n_t),
        dma(n_o), dma(n_o), pltpu.SemaphoreType.DMA, dma(n_o), dma(n_layers), dma(n_layers, n_o), dma(n_layers), dma(n_layers), dma(2),
        dma(2), dma(2, 2, RING), dma(RING), dma(*pair), dma(2, 2), dma(*pair), dma(2, 2),
        dma(3), dma(n_layers, n_o), dma(n_layers, n_o), dma(n_layers),
    ]
    res = pl.pallas_call(
        model_kernel,
        out_shape=out_shape,
        in_specs=[any_spec] * 7,
        out_specs=[any_spec] * len(out_shape),
        scratch_shapes=scratch,
        compiler_params=pltpu.CompilerParams(collective_id=0, has_side_effects=True, vmem_limit_bytes=VMEM_LIMIT),
        name="two_layers",
    )(xt, gain, wkv_t, w_in, w_out, cos_full, sin_full)
    return res[0], res[6]


def solution(mesh):
    row_size = mesh.shape["row"]
    n_col = mesh.shape["col"]
    n_z = row_size // RING
    n_y = RING
    n_x = n_col // CORES
    n_tp = n_y * n_col
    n_dev = row_size * n_col
    mesh4 = Mesh(mesh.devices.reshape(n_z, n_y, n_x, CORES), ("z", "y", "x", "core"))
    every = ("z", "y", "x", "core")
    col = ("x", "core")
    act_spec = P(NIL, NIL, every)
    w_spec = P(NIL, ("z", "y"), col)

    def device_fn(x_loc, gain_loc, w_in_loc, w_kv_loc, w_out_loc):
        n_layers = w_in_loc.shape[0]
        n_batch, seq_len, d_local = x_loc.shape
        head_dim = w_kv_loc.shape[2] * n_col // 2
        batch_loc = n_batch // n_z
        seq_local = seq_len // n_dev
        steps = np.arange(head_dim // 2, dtype=np.float32)
        inv_freq = (1.0 / 10000.0 ** (steps * 2 / head_dim)).astype(np.float32)
        angles = np.arange(seq_len, dtype=np.float32)[:, NIL] * inv_freq[NIL, :]
        cos_tab, sin_tab = np.cos(angles), np.sin(angles)
        cos_full = jnp.asarray(np.concatenate([cos_tab, cos_tab], axis=1))
        sin_full = jnp.asarray(np.concatenate([-sin_tab, sin_tab], axis=1))
        y_loc, kv = run_model(x_loc.transpose(0, 2, 1), gain_loc, w_kv_loc.transpose(0, 2, 1), w_in_loc, w_out_loc, cos_full, sin_full)
        y_loc = y_loc.transpose(0, 2, 1)
        kv = kv.reshape(n_layers, n_z, 2, batch_loc, CORES, seq_local, head_dim)
        kv = lax.dynamic_index_in_dim(kv, lax.axis_index("core"), axis=4, keepdims=False)
        kv = kv.transpose(0, 2, 1, 3, 4, 5).reshape(n_layers, 2, n_batch, seq_local, head_dim)
        return y_loc, kv

    return jax.shard_map(device_fn, mesh=mesh4, in_specs=(act_spec, P(NIL, every), w_spec, w_spec, P(NIL, col, ("z", "y"))), out_specs=(act_spec, P(NIL, NIL, NIL, every, NIL)), check_vma=False)
```

profile of v0, /device:TPU:1, one launch (start us, length us, event | category | flops | bytes accessed | tf_op | source)
XLA Modules:
  0.0 327.6 jit_solution(543068141574795681)
XLA Ops:
  0.6 323.5 %two_layers.1 = (bf16[16,32,512]{2,1,0:T(8,128)(2,1)}, bf16[2,2,4,512,128]{4,3,2,1,0:T(8,128)(2,1)}, bf16[2,4,4,2,64,4096]{5,4,3,2,1,0:T(8,128)(2,1)}, bf16[2,4,...) custom-call(bf16[16,32,512]{2,1,0:T(8,128)(2,1)} %bitcast.11, ...), custom_call_target="tpu_custom_call" | custom-call | tf_op jit(solution)/shard_map/two_layers/pallas_call | solution.py:1247
  324.2 0.9 dynamic-slice_bitcast_fusion
  325.1 0.7 copy.12
  325.7 1.9 copy.15
  (1 shorter events, 0.0 us)
where the time goes:
time: 328 us
  Pallas kernels  324 us (99%)
  local copies, waits for them, and re-layouts  3.43 us (1%)
    pallas_call x1, Pallas kernels, run_model(): pl.pallas_call(model_kernel, out_shape=out_shape, in_specs=[any_spec] * 7...  324 us

commit v1 on v0

--- a/solution.py
+++ b/solution.py
@@ -836,8 +836,6 @@
             kv_out_copy(l, s, pair, i).start()
         q = project(h_tile(slot), 0, head_dim)
         r.stage[...] = (rope(q) * head_dim ** -0.5).astype(BF)
-        for lo in range(0, f_loc, n_chunk):
-            r.joined[s, :, head_dim + lo:head_dim + lo + n_chunk] = project(h_tile(slot), head_dim + lo, n_chunk)
         n_tile = seq_len // 2
         for i in BOTH:
             keys = (i + 1) * n_tile
@@ -850,6 +848,8 @@
             prob = (ex * (1.0 / jnp.sum(ex, axis=-1, keepdims=True))).astype(BF)
             att = jnp.dot(prob, r.qkv[pair, 1, :keys, :], preferred_element_type=F32)
             r.joined[s, i * n_tile:(i + 1) * n_tile, :head_dim] = att.astype(BF)
+        for lo in range(0, f_loc, n_chunk):
+            r.joined[s, :, head_dim + lo:head_dim + lo + n_chunk] = project(h_tile(slot), head_dim + lo, n_chunk)
 
     def h_cols(slot, col, n):
         return r.hb[slot, :, :, :, col:col + n].reshape(seq_len, n)

time: 328 us -> 330 us (level)
  no operation moved by 1% of the time
where the time goes in v1:
time: 330 us; the launch traced here: 329 us
  Pallas kernels  325 us (98%)
  local copies, waits for them, and re-layouts  3.43 us (1%)
    pallas_call x1, Pallas kernels, run_model(): pl.pallas_call(model_kernel, out_shape=out_shape, in_specs=[any_spec] * 7...  325 us

profile of v1, /device:TPU:1, one launch (start us, length us, event | category | flops | bytes accessed | tf_op | source)
XLA Modules:
  0.0 329.2 jit_solution(405545022526690138)
XLA Ops:
  0.6 325.1 %two_layers.1 = (bf16[16,32,512]{2,1,0:T(8,128)(2,1)}, bf16[2,2,4,512,128]{4,3,2,1,0:T(8,128)(2,1)}, bf16[2,4,4,2,64,4096]{5,4,3,2,1,0:T(8,128)(2,1)}, bf16[2,4,...) custom-call(bf16[16,32,512]{2,1,0:T(8,128)(2,1)} %bitcast.11, ...), custom_call_target="tpu_custom_call" | custom-call | tf_op jit(solution)/shard_map/two_layers/pallas_call | solution.py:1247
  325.7 0.9 dynamic-slice_bitcast_fusion
  326.6 0.7 copy.12
  327.3 1.9 copy.15
  (1 shorter events, 0.0 us)

commit v2 on v0

--- a/solution.py
+++ b/solution.py
@@ -561,10 +561,10 @@
 
     def kv_trade(l, k):
         zz = turn(z, OTHERS[k])
-        return remote(r.kv_out.at[l, :, :, kv_rows(zz)], r.kvx.at[l, z], r.kvx_send.at[l, k], r.kvx_recv.at[l, k], (zz, y, x, c))
+        return remote(r.kv_out.at[l, :, :, kv_rows(zz)], r.kvx.at[l, :, pl.ds(z * seqs, seqs)], r.kvx_send.at[l, k], r.kvx_recv.at[l, k], (zz, y, x, c))
 
     def kv_keep(l):
-        return pltpu.make_async_copy(r.kv_out.at[l, :, :, kv_rows(z)], r.kvx.at[l, z], r.kvx_loc.at[l])
+        return pltpu.make_async_copy(r.kv_out.at[l, :, :, kv_rows(z)], r.kvx.at[l, :, pl.ds(z * seqs, seqs)], r.kvx_loc.at[l])
 
     def kv_share(l):
         for k in range(len(OTHERS)):
@@ -1219,7 +1219,7 @@
         out(n_layers, RING, RING * d_row, e_loc),
         out(n_layers, RING, RING, r_loc, d_col),
         out(RING, CORES, n_layers, RING, RING, kc, d_row),
-        out(n_layers, RING, 2, seqs, CORES * (seq_len // (CORES * RING * RING * RING)), head_dim),
+        out(n_layers, 2, batch, CORES * (seq_len // (CORES * RING * RING * RING)), head_dim),
         out(n_layers, 2, d_row // 2, e_loc),
         out(n_layers, 2, r_loc // 2, d_col),
     ]
@@ -1284,9 +1284,8 @@
         sin_full = jnp.asarray(np.concatenate([-sin_tab, sin_tab], axis=1))
         y_loc, kv = run_model(x_loc.transpose(0, 2, 1), gain_loc, w_kv_loc.transpose(0, 2, 1), w_in_loc, w_out_loc, cos_full, sin_full)
         y_loc = y_loc.transpose(0, 2, 1)
-        kv = kv.reshape(n_layers, n_z, 2, batch_loc, CORES, seq_local, head_dim)
-        kv = lax.dynamic_index_in_dim(kv, lax.axis_index("core"), axis=4, keepdims=False)
-        kv = kv.transpose(0, 2, 1, 3, 4, 5).reshape(n_layers, 2, n_batch, seq_local, head_dim)
+        kv = kv.reshape(n_layers, 2, n_batch, CORES, seq_local, head_dim)
+        kv = lax.dynamic_index_in_dim(kv, lax.axis_index("core"), axis=3, keepdims=False)
         return y_loc, kv
 
     return jax.shard_map(device_fn, mesh=mesh4, in_specs=(act_spec, P(NIL, every), w_spec, w_spec, P(NIL, col, ("z", "y"))), out_specs=(act_spec, P(NIL, NIL, NIL, every, NIL)), check_vma=False)

time: 328 us -> 328 us (level)
  no operation moved by 1% of the time
where the time goes in v2:
time: 328 us
  Pallas kernels  324 us (99%)
  local copies, waits for them, and re-layouts  3.38 us (1%)
    pallas_call x1, Pallas kernels, run_model(): pl.pallas_call(model_kernel, out_shape=out_shape, in_specs=[any_spec] * 7...  324 us

profile of v2, /device:TPU:1, one launch (start us, length us, event | category | flops | bytes accessed | tf_op | source)
XLA Modules:
  0.0 327.8 jit_solution(12448681928795175149)
XLA Ops:
  0.6 323.8 %two_layers.1 = (bf16[16,32,512]{2,1,0:T(8,128)(2,1)}, bf16[2,2,4,512,128]{4,3,2,1,0:T(8,128)(2,1)}, bf16[2,4,4,2,64,4096]{5,4,3,2,1,0:T(8,128)(2,1)}, bf16[2,4,...) custom-call(bf16[16,32,512]{2,1,0:T(8,128)(2,1)} %bitcast.6, ...), custom_call_target="tpu_custom_call" | custom-call | tf_op jit(solution)/shard_map/two_layers/pallas_call | solution.py:1247
  324.4 1.5 dynamic-slice_bitcast_fusion
  325.9 1.9 copy.10

commit v3 on v0

--- a/solution.py
+++ b/solution.py
@@ -414,7 +414,7 @@
 
     def gain_die(xx, k):
         ref = r.gbuf.at[xx, c]
-        return remote(ref, ref, r.gd_send.at[k], r.gd_recv.at[k], partner)
+        return remote(ref, ref, r.gd_send, r.gd_recv, partner)
 
     def gain_sum():
         for zz in RINGS:
@@ -477,8 +477,8 @@
         three_planes().wait_send()
         for fn in (gain_z, gain_y, gain_x):
             peers_of(fn, "wait_send")
-        for k in RINGS:
-            gain_die(x, k).wait_send()
+        ref = r.gbuf.at[:, c]
+        remote(ref, ref, r.gd_send, r.gd_recv, partner).wait_send()
         for oy in RINGS:
             got = row_bytes(oy)
             remote(got, got, r.xp_send.at[oy], r.xp_recv.at[oy], partner).wait_send()
@@ -561,7 +561,7 @@
 
     def kv_trade(l, k):
         zz = turn(z, OTHERS[k])
-        return remote(r.kv_out.at[l, :, :, kv_rows(zz)], r.kvx.at[l, z], r.kvx_send.at[l, k], r.kvx_recv.at[l, k], (zz, y, x, c))
+        return remote(r.kv_out.at[l, :, :, kv_rows(zz)], r.kvx.at[l, z], r.kvx_send.at[l], r.kvx_recv.at[l], (zz, y, x, c))
 
     def kv_keep(l):
         return pltpu.make_async_copy(r.kv_out.at[l, :, :, kv_rows(z)], r.kvx.at[l, z], r.kvx_loc.at[l])
@@ -572,8 +572,8 @@
         kv_keep(l).start()
 
     def kv_shared(l):
-        for k in range(len(OTHERS)):
-            kv_trade(l, k).wait()
+        ref = r.kvx.at[l, pl.ds(0, LAST)]
+        remote(ref, ref, r.kvx_send.at[l], r.kvx_recv.at[l], here).wait()
         kv_keep(l).wait()
 
     def gather_norm(l, split, pump):
@@ -1074,8 +1074,8 @@
         kv_y3()
         pump("s6")
         with jax.named_scope("gain_sum"):
-            for k in RINGS:
-                gain_die(x, k).wait_recv()
+            ref = r.gbuf.at[:, 1 - c]
+            remote(ref, ref, r.gd_send, r.gd_recv, partner).wait_recv()
             gain_sum()
             for fill in fills[1:]:
                 fill.wait()
@@ -1236,13 +1236,13 @@
         vm(*pair, 2, rows, width), vm(*pair, RING, rows, width), vm(*pair, rows // 2, width), vm(*pair, rows, width),
         pltpu.SemaphoreType.DMA, pltpu.SemaphoreType.DMA, dma(RING), dma(RING), pltpu.SemaphoreType.DMA, pltpu.SemaphoreType.DMA,
         pltpu.SemaphoreType.DMA,
-        dma(3 * n_o), dma(3 * n_o), dma(RING), dma(RING),
+        dma(3 * n_o), dma(3 * n_o), pltpu.SemaphoreType.DMA, pltpu.SemaphoreType.DMA,
         dma(RING), dma(RING), dma(2, RING), dma(2, RING), dma(RING), dma(RING), pltpu.SemaphoreType.DMA,
         dma(RING), dma(40), pltpu.SemaphoreType.DMA, dma(RING), pltpu.SemaphoreType.DMA, dma(H_SLOTS), dma(2, 2), dma(3), dma(3),
         dma(n_t, RING), dma(n_t, 2), dma(3, RING, 2), dma(3), dma(n_t),
         dma(n_o), dma(n_o), pltpu.SemaphoreType.DMA, dma(n_o), dma(n_layers), dma(n_layers, n_o), dma(n_layers), dma(n_layers), dma(2),
         dma(2), dma(2, 2, RING), dma(RING), dma(*pair), dma(2, 2), dma(*pair), dma(2, 2),
-        dma(3), dma(n_layers, n_o), dma(n_layers, n_o), dma(n_layers),
+        dma(3), dma(n_layers), dma(n_layers), dma(n_layers),
     ]
     res = pl.pallas_call(
         model_kernel,

time: 328 us -> 328 us (level)
  no operation moved by 1% of the time
where the time goes in v3:
time: 328 us; the launch traced here: 327 us
  Pallas kernels  323 us (98%)
  local copies, waits for them, and re-layouts  3.43 us (1%)
    pallas_call x1, Pallas kernels, run_model(): pl.pallas_call(model_kernel, out_shape=out_shape, in_specs=[any_spec] * 7...  323 us

profile of v3, /device:TPU:1, one launch (start us, length us, event | category | flops | bytes accessed | tf_op | source)
XLA Modules:
  0.0 327.5 jit_solution(7949491785676188299)
XLA Ops:
  0.6 323.4 %two_layers.1 = (bf16[16,32,512]{2,1,0:T(8,128)(2,1)}, bf16[2,2,4,512,128]{4,3,2,1,0:T(8,128)(2,1)}, bf16[2,4,4,2,64,4096]{5,4,3,2,1,0:T(8,128)(2,1)}, bf16[2,4,...) custom-call(bf16[16,32,512]{2,1,0:T(8,128)(2,1)} %bitcast.11, ...), custom_call_target="tpu_custom_call" | custom-call | tf_op jit(solution)/shard_map/two_layers/pallas_call | solution.py:1247
  324.0 0.9 dynamic-slice_bitcast_fusion
  324.9 0.7 copy.12
  325.6 1.9 copy.15
  (1 shorter events, 0.0 us)
